TPU v7x, 32 devices: a whole 2x2x4 slice. The times are simulated.
32 devices in a mesh: row: 16 (over z, y, x), col: 2 (over core).
Axes of the slice: x: 2, y: 2, z: 4, core: 2. Of those that a mesh axis runs over, the one named last changes fastest.
Arguments:
- adj_tiles: bfloat16 [16, 2, 128, 128, 128], P('row', 'col'), may hold values from 0 to 1, as said below
- tile_rows: int32 [16, 2, 128], P('row', 'col'), may hold values from 0 to 1, as said below
- tile_cols: int32 [16, 2, 128], P('row', 'col'), may hold values from 0 to 15, as said below
- tile_count: int32 [16, 2], P('row', 'col'), may hold values from 1 to 128, as said below
- tile_depth: int32 [32, 128], P(('row', 'col')), may hold values from 1 to 7, as said below
- source_ids: int32 [128], replicated, may hold values from 0 to 4095
Outputs:
- path_sums: float32 [4096, 128], P(('row', 'col'))
- log_scales: float32 [6, 128], replicated
Inputs may be any that keep to these rules, and one draw needn't show every extreme that they name: `adj_tiles`: every entry is 0 or 1. The live slots of a device are its first tile_count slots; at least one device holds 128 live slots. `tile_rows`: slots past a device's live count carry 0. `tile_cols`: slots past a device's live count carry 0. `tile_depth`: the value 6 + 1 marks a tile that takes path counts at every level.
All inputs are finite; a program needn't handle non-finite values.
Results may differ from a plain program's by a relative error of at most 0.0003.
Values may be sent and summed in bfloat16 or wider, within the bound.
A program may use at most 64 MiB of HBM per device.

v0:
```python
import jax
import jax.numpy as jnp
from jax import lax
from jax.sharding import PartitionSpec as P

TILE = 128
LEVELS = 6


EPSILON = 1e-06


def tile_products(running, blocks, row_ids, col_ids, sources, first_slot, end_slot):
    slot_total = blocks.shape[0]
    batch_size = min(16, slot_total)
    turn_count = (jnp.maximum(end_slot - first_slot, 0) + batch_size - 1) // batch_size

    def one_turn(turn_index, summed):
        wanted_start = first_slot + turn_index * batch_size
        window = jnp.minimum(wanted_start, slot_total - batch_size)
        part_blocks = lax.dynamic_slice_in_dim(blocks, window, batch_size, 0)
        part_rows = lax.dynamic_slice_in_dim(row_ids, window, batch_size, 0)
        part_cols = lax.dynamic_slice_in_dim(col_ids, window, batch_size, 0)
        slot_ids = window + jnp.arange(batch_size, dtype=jnp.int32)
        wanted = (slot_ids >= wanted_start) & (slot_ids < end_slot)
        local_cols = jnp.clip(part_cols, 0, sources.shape[0] - 1)
        picked = jnp.take(sources, local_cols, axis=0)
        products = jnp.einsum(
            "gij,gjs->gis", part_blocks, picked, preferred_element_type=jnp.float32
        )
        return summed.at[part_rows].add(products * wanted.astype(jnp.float32)[:, None, None])

    return lax.fori_loop(0, turn_count, one_turn, running)


def ordered_list(tile_list, src_tiles):
    blocks, row_ids, col_ids, live_count = tile_list
    slot_ids = jnp.arange(blocks.shape[0], dtype=jnp.int32)
    sort_keys = jnp.where(slot_ids < live_count, col_ids, src_tiles)
    slot_order = jnp.argsort(sort_keys, stable=True)
    return (
        jnp.take(blocks, slot_order, axis=0),
        jnp.take(row_ids, slot_order),
        jnp.take(sort_keys, slot_order),
        live_count,
    )


def local(adj_tiles, tile_rows, tile_cols, tile_count, tile_depth, source_ids):
    blocks = adj_tiles[0, 0]
    row_ids = tile_rows[0, 0]
    col_ids = tile_cols[0, 0]
    live_count = tile_count[0, 0]
    row_total = lax.axis_size("row")
    col_total = lax.axis_size("col")
    piece_tiles = tile_depth.shape[0]
    panel_width = tile_depth.shape[1]
    piece_rows = piece_tiles * TILE
    dest_tiles = col_total * piece_tiles
    src_tiles = row_total * piece_tiles
    vertex_total = piece_rows * row_total * col_total
    position = lax.axis_index("row") * col_total + lax.axis_index("col")
    vertex_ids = position * piece_rows + jnp.arange(piece_rows, dtype=jnp.int32)
    start_panel = (vertex_ids[:, None] == source_ids[None, :]).astype(jnp.float32)
    tile_lists = [(blocks, row_ids, col_ids, live_count)]
    tile_lists = [ordered_list(tile_list, src_tiles) for tile_list in tile_lists]
    zero_sums = jnp.zeros((dest_tiles, TILE, panel_width), jnp.float32)
    path_sums = start_panel
    frontier = start_panel.astype(jnp.bfloat16)
    log_scales = []
    for level_index in range(1, LEVELS + 1):
        carried = tuple((zero_sums for tile_list in tile_lists))
        piece_block = lax.all_gather(frontier, "row", axis=0, tiled=True)
        count_tiles = piece_block.shape[0] // TILE
        sources = piece_block.reshape(count_tiles, TILE, panel_width)
        base_tile = jnp.int32(0) // TILE
        updated = []
        for fold_tile_list, running in zip(tile_lists, carried):
            first_slot = jnp.sum((fold_tile_list[2] < base_tile).astype(jnp.int32))
            end_slot = jnp.sum((fold_tile_list[2] < base_tile + count_tiles).astype(jnp.int32))
            updated.append(
                tile_products(
                    running,
                    fold_tile_list[0],
                    fold_tile_list[1],
                    fold_tile_list[2],
                    sources,
                    first_slot,
                    end_slot,
                )
            )
        partials = tuple(updated)
        combined = partials[0]
        reduced = lax.psum_scatter(
            combined.reshape(dest_tiles * TILE, panel_width), "col", scatter_dimension=0, tiled=True
        )
        reached = (tile_depth >= level_index).astype(jnp.float32)
        raw_paths = (reduced.reshape(piece_tiles, TILE, panel_width) * reached[:, None, :]).reshape(
            piece_rows, panel_width
        )
        squares = lax.psum(jnp.sum(raw_paths * raw_paths, axis=0), ("row", "col"))
        mean_square = squares / vertex_total + EPSILON
        scaled = raw_paths * lax.rsqrt(mean_square)
        path_sums = path_sums + scaled
        log_scales.append(0.5 * jnp.log(mean_square))
        frontier = scaled.astype(jnp.bfloat16)
    return (path_sums, jnp.stack(log_scales))


def solution(mesh):
    in_specs = (
        P("row", "col", None, None, None),
        P("row", "col", None),
        P("row", "col", None),
        P("row", "col"),
        P(("row", "col"), None),
        P(),
    )
    out_specs = (P(("row", "col"), None), P())
    return jax.shard_map(local, mesh=mesh, in_specs=in_specs, out_specs=out_specs, check_vma=False)
```

profile of v0, /device:TPU:0, one launch (start us, length us, event | category | flops | bytes accessed | tf_op | source)
XLA Modules:
  0.0 806.0 jit_solution(13640891762177234601)
XLA Ops:
  25.5 45.3 %all_gather.18 = bf16[2048,128]{1,0:T(8,128)(2,1)S(1)} all-gather(bf16[128,128]{1,0:T(8,128)(2,1)S(1)} %convert_convert_fusion), channel_id=1, replica_groups=mesh['row'=16,'col'=2] {'row'}, dimensions={0}, use_global_device_ids=true | all-gather | bytes 557056 | tf_op jit(solution)/shard_map/all_gather | solution.py:73
  70.8 20.7 %while.60 = (s32[]{:T(128)}, f32[2,128,128]{2,1,0:T(8,128)S(1)}, s32[]{:T(128)}, s32[]{:T(128)}, s32[128]{0:T(128)S(1)}, /*index=5*/bf16[128,128,128]{2,1,0:T(8,...) while((s32[]{:T(128)}, f32[2,128,128]{2,1,0:T(8,128)S(1)}, ...), condition=%wide.region_5.8_spmd, body=%wide.region_3.7_spmd.sunk | while | flops 67896568 | bytes 6296387 | solution.py:33
  92.2 22.0 %reduce-scatter.7.cloned.1.call-done = f32[128,128]{1,0:T(8,128)} async-done(((f32[256,128]{1,0:T(8,128)}), f32[128,128]{1,0:T(8,128)}) %reduce-scatter.7.cloned.1.call-update) | async-done | bytes 65552 | tf_op jit(solution)/shard_map/reduce_scatter | solution.py:94
  115.1 40.4 %psum.42 = f32[128]{0:T(128)S(1)} all-reduce(f32[128]{0:T(128)S(1)} %multiply_reduce_fusion.5), channel_id=1, replica_groups=mesh['row'=16,'col'=2] {'row','col'}, use_global_device_ids=true, to_apply=%region_8.11 | all-reduce | flops 128 | bytes 1024 | tf_op jit(solution)/shard_map/psum | solution.py:101
  156.4 42.6 %all_gather.19 = bf16[2048,128]{1,0:T(8,128)(2,1)S(1)} all-gather(bf16[128,128]{1,0:T(8,128)(2,1)S(1)} %multiply_convert_fusion.4), channel_id=1, replica_groups=mesh['row'=16,'col'=2] {'row'}, dimensions={0}, use_global_device_ids=true | all-gather | bytes 557056 | tf_op jit(solution)/shard_map/all_gather | solution.py:73
  199.0 20.7 %while.61 = (s32[]{:T(128)}, f32[2,128,128]{2,1,0:T(8,128)S(1)}, s32[]{:T(128)}, s32[]{:T(128)}, s32[128]{0:T(128)S(1)}, /*index=5*/bf16[128,128,128]{2,1,0:T(8,...) while((s32[]{:T(128)}, f32[2,128,128]{2,1,0:T(8,128)S(1)}, ...), condition=%wide.region_11.14_spmd, body=%wide.region_9.13_spmd.sunk | while | flops 67896568 | bytes 6296387 | solution.py:33
  220.4 22.0 %reduce-scatter.9.cloned.1.call-done = f32[128,128]{1,0:T(8,128)} async-done(((f32[256,128]{1,0:T(8,128)}), f32[128,128]{1,0:T(8,128)}) %reduce-scatter.9.cloned.1.call-update) | async-done | bytes 65552 | tf_op jit(solution)/shard_map/reduce_scatter | solution.py:94
  243.3 40.4 %psum.43 = f32[128]{0:T(128)S(1)} all-reduce(f32[128]{0:T(128)S(1)} %multiply_reduce_fusion.4), channel_id=1, replica_groups=mesh['row'=16,'col'=2] {'row','col'}, use_global_device_ids=true, to_apply=%region_14.17 | all-reduce | flops 128 | bytes 1024 | tf_op jit(solution)/shard_map/psum | solution.py:101
  284.5 42.7 %all_gather.20 = bf16[2048,128]{1,0:T(8,128)(2,1)S(1)} all-gather(bf16[128,128]{1,0:T(8,128)(2,1)S(1)} %multiply_convert_fusion.3), channel_id=1, replica_groups=mesh['row'=16,'col'=2] {'row'}, dimensions={0}, use_global_device_ids=true | all-gather | bytes 557056 | tf_op jit(solution)/shard_map/all_gather | solution.py:73
  327.3 20.7 %while.62 = (s32[]{:T(128)}, f32[2,128,128]{2,1,0:T(8,128)S(1)}, s32[]{:T(128)}, s32[]{:T(128)}, s32[128]{0:T(128)S(1)}, /*index=5*/bf16[128,128,128]{2,1,0:T(8,...) while((s32[]{:T(128)}, f32[2,128,128]{2,1,0:T(8,128)S(1)}, ...), condition=%wide.region_17.20_spmd, body=%wide.region_15.19_spmd.sunk | while | flops 67896568 | bytes 6296387 | solution.py:33
  348.7 22.0 %reduce-scatter.11.cloned.1.call-done = f32[128,128]{1,0:T(8,128)} async-done(((f32[256,128]{1,0:T(8,128)}), f32[128,128]{1,0:T(8,128)}) %reduce-scatter.11.cloned.1.call-update) | async-done | bytes 65552 | tf_op jit(solution)/shard_map/reduce_scatter | solution.py:94
  371.5 40.4 %psum.44 = f32[128]{0:T(128)S(1)} all-reduce(f32[128]{0:T(128)S(1)} %multiply_reduce_fusion.3), channel_id=1, replica_groups=mesh['row'=16,'col'=2] {'row','col'}, use_global_device_ids=true, to_apply=%region_20.23 | all-reduce | flops 128 | bytes 1024 | tf_op jit(solution)/shard_map/psum | solution.py:101
  412.8 42.6 %all_gather.21 = bf16[2048,128]{1,0:T(8,128)(2,1)S(1)} all-gather(bf16[128,128]{1,0:T(8,128)(2,1)S(1)} %multiply_convert_fusion.2), channel_id=1, replica_groups=mesh['row'=16,'col'=2] {'row'}, dimensions={0}, use_global_device_ids=true | all-gather | bytes 557056 | tf_op jit(solution)/shard_map/all_gather | solution.py:73
  455.5 20.7 %while.63 = (s32[]{:T(128)}, f32[2,128,128]{2,1,0:T(8,128)S(1)}, s32[]{:T(128)}, s32[]{:T(128)}, s32[128]{0:T(128)S(1)}, /*index=5*/bf16[128,128,128]{2,1,0:T(8,...) while((s32[]{:T(128)}, f32[2,128,128]{2,1,0:T(8,128)S(1)}, ...), condition=%wide.region_23.26_spmd, body=%wide.region_21.25_spmd.sunk | while | flops 67896568 | bytes 6296387 | solution.py:33
  476.9 22.0 %reduce-scatter.13.cloned.1.call-done = f32[128,128]{1,0:T(8,128)} async-done(((f32[256,128]{1,0:T(8,128)}), f32[128,128]{1,0:T(8,128)}) %reduce-scatter.13.cloned.1.call-update) | async-done | bytes 65552 | tf_op jit(solution)/shard_map/reduce_scatter | solution.py:94
  499.7 40.4 %psum.45 = f32[128]{0:T(128)S(1)} all-reduce(f32[128]{0:T(128)S(1)} %multiply_reduce_fusion.2), channel_id=1, replica_groups=mesh['row'=16,'col'=2] {'row','col'}, use_global_device_ids=true, to_apply=%region_26.29 | all-reduce | flops 128 | bytes 1024 | tf_op jit(solution)/shard_map/psum | solution.py:101
  541.0 42.6 %all_gather.22 = bf16[2048,128]{1,0:T(8,128)(2,1)S(1)} all-gather(bf16[128,128]{1,0:T(8,128)(2,1)S(1)} %multiply_convert_fusion.1), channel_id=1, replica_groups=mesh['row'=16,'col'=2] {'row'}, dimensions={0}, use_global_device_ids=true | all-gather | bytes 557056 | tf_op jit(solution)/shard_map/all_gather | solution.py:73
  583.7 20.9 %while.64 = (s32[]{:T(128)}, f32[2,128,128]{2,1,0:T(8,128)S(1)}, s32[]{:T(128)}, s32[]{:T(128)}, s32[128]{0:T(128)S(1)}, /*index=5*/bf16[128,128,128]{2,1,0:T(8,...) while((s32[]{:T(128)}, f32[2,128,128]{2,1,0:T(8,128)S(1)}, ...), condition=%wide.region_29.32_spmd, body=%wide.region_27.31_spmd.sunk | while | flops 67896568 | bytes 6296387 | solution.py:33
  605.2 22.0 %reduce-scatter.15.cloned.1.call-done = f32[128,128]{1,0:T(8,128)} async-done(((f32[256,128]{1,0:T(8,128)}), f32[128,128]{1,0:T(8,128)}) %reduce-scatter.15.cloned.1.call-update) | async-done | bytes 65552 | tf_op jit(solution)/shard_map/reduce_scatter | solution.py:94
  628.1 40.4 %psum.46 = f32[128]{0:T(128)S(1)} all-reduce(f32[128]{0:T(128)S(1)} %multiply_reduce_fusion.1), channel_id=1, replica_groups=mesh['row'=16,'col'=2] {'row','col'}, use_global_device_ids=true, to_apply=%region_32.35 | all-reduce | flops 128 | bytes 1024 | tf_op jit(solution)/shard_map/psum | solution.py:101
  669.4 42.7 %all_gather.23 = bf16[2048,128]{1,0:T(8,128)(2,1)S(1)} all-gather(bf16[128,128]{1,0:T(8,128)(2,1)S(1)} %multiply_convert_fusion), channel_id=1, replica_groups=mesh['row'=16,'col'=2] {'row'}, dimensions={0}, use_global_device_ids=true | all-gather | bytes 557056 | tf_op jit(solution)/shard_map/all_gather | solution.py:73
  712.1 20.8 %while.65 = (s32[]{:T(128)}, f32[2,128,128]{2,1,0:T(8,128)S(1)}, s32[]{:T(128)}, s32[]{:T(128)}, s32[128]{0:T(128)S(1)}, /*index=5*/bf16[128,128,128]{2,1,0:T(8,...) while((s32[]{:T(128)}, f32[2,128,128]{2,1,0:T(8,128)S(1)}, ...), condition=%wide.region_35.38_spmd, body=%wide.region_33.37_spmd.sunk | while | flops 67896568 | bytes 6296387 | solution.py:33
  733.6 22.0 %reduce-scatter.17.cloned.1.call-done = f32[128,128]{1,0:T(8,128)} async-done(((f32[256,128]{1,0:T(8,128)}), f32[128,128]{1,0:T(8,128)}) %reduce-scatter.17.cloned.1.call-update) | async-done | bytes 65552 | tf_op jit(solution)/shard_map/reduce_scatter | solution.py:94
  756.5 40.4 %psum.47 = f32[128]{0:T(128)S(1)} all-reduce(f32[128]{0:T(128)S(1)} %multiply_reduce_fusion), channel_id=1, replica_groups=mesh['row'=16,'col'=2] {'row','col'}, use_global_device_ids=true, to_apply=%region_38.41 | all-reduce | flops 128 | bytes 1024 | tf_op jit(solution)/shard_map/psum | solution.py:101
  (223 shorter events, 139.5 us)
Async XLA Ops:
  7.2 5.2 copy-start
  7.2 107.0 %reduce-scatter.7.cloned.1.call-start = ((), (), s32[]{:S(2)}) async-start(), calls=%async_computation.6 | async-start | bytes 196608 | tf_op jit(solution)/shard_map/reduce_scatter | solution.py:94
  20.8 4.6 copy-start.12
  70.8 21.4 %copy-start.13 = (s32[1,128]{1,0:T(1,128)S(1)}, s32[1,128]{1,0:T(1,128)}, u32[]{:S(2)}) copy-start(s32[1,128]{1,0:T(1,128)} %param.26) | copy-start | bytes 1540
  91.5 0.6 copy-start.2
  92.2 150.2 %reduce-scatter.9.cloned.1.call-start = ((), (), s32[]{:S(2)}) async-start(), calls=%async_computation.7 | async-start | bytes 196608 | tf_op jit(solution)/shard_map/reduce_scatter | solution.py:94
  219.7 0.6 copy-start.3
  220.4 150.3 %reduce-scatter.11.cloned.1.call-start = ((), (), s32[]{:S(2)}) async-start(), calls=%async_computation.8 | async-start | bytes 196608 | tf_op jit(solution)/shard_map/reduce_scatter | solution.py:94
  347.9 0.6 copy-start.4
  348.6 150.3 %reduce-scatter.13.cloned.1.call-start = ((), (), s32[]{:S(2)}) async-start(), calls=%async_computation.9 | async-start | bytes 196608 | tf_op jit(solution)/shard_map/reduce_scatter | solution.py:94
  476.1 0.6 copy-start.5
  476.8 150.4 %reduce-scatter.15.cloned.1.call-start = ((), (), s32[]{:S(2)}) async-start(), calls=%async_computation.10 | async-start | bytes 196608 | tf_op jit(solution)/shard_map/reduce_scatter | solution.py:94
  604.5 0.6 copy-start.6
  605.2 150.4 %reduce-scatter.17.cloned.1.call-start = ((), (), s32[]{:S(2)}) async-start(), calls=%async_computation.11 | async-start | bytes 196608 | tf_op jit(solution)/shard_map/reduce_scatter | solution.py:94
  712.1 85.5 %copy-start.7 = (f32[128,128]{1,0:T(8,128)S(1)}, f32[128,128]{1,0:T(8,128)}, u32[]{:S(2)}) copy-start(f32[128,128]{1,0:T(8,128)} %reduce-scatter.7.cloned.1.call-done) | copy-start | bytes 196612
  712.1 85.4 %copy-start.8 = (f32[128,128]{1,0:T(8,128)S(1)}, f32[128,128]{1,0:T(8,128)}, u32[]{:S(2)}) copy-start(f32[128,128]{1,0:T(8,128)} %reduce-scatter.9.cloned.1.call-done) | copy-start | bytes 196612
  712.1 85.4 %copy-start.9 = (f32[128,128]{1,0:T(8,128)S(1)}, f32[128,128]{1,0:T(8,128)}, u32[]{:S(2)}) copy-start(f32[128,128]{1,0:T(8,128)} %reduce-scatter.11.cloned.1.call-done) | copy-start | bytes 196612
  712.1 85.4 %copy-start.10 = (f32[128,128]{1,0:T(8,128)S(1)}, f32[128,128]{1,0:T(8,128)}, u32[]{:S(2)}) copy-start(f32[128,128]{1,0:T(8,128)} %reduce-scatter.13.cloned.1.call-done) | copy-start | bytes 196612
  712.1 85.4 %copy-start.11 = (f32[128,128]{1,0:T(8,128)S(1)}, f32[128,128]{1,0:T(8,128)}, u32[]{:S(2)}) copy-start(f32[128,128]{1,0:T(8,128)} %reduce-scatter.15.cloned.1.call-done) | copy-start | bytes 196612
  732.9 0.6 copy-start.1
Sparse Core Ops, SparseCore 0:
  92.3 21.8 reduce-scatter.6
  220.5 21.8 reduce-scatter.8
  348.7 21.8 reduce-scatter.10
  476.9 21.8 reduce-scatter.12
  605.3 21.8 reduce-scatter.14
  733.7 21.8 reduce-scatter.16
where the time goes:
time: 810 us; the launch traced here: 806 us
  blocking collectives  501 us (62%)
  waiting for transfers between devices  132 us (16%)
  other arithmetic  77.3 us (10%)
  matrix products  34.1 us (4%)
  local copies, waits for them, and re-layouts  27.7 us (3%)
  loops' own time  17.1 us (2%)
  between operations  16.3 us (2%)
    all_gather x6, blocking collectives, local(): piece_block = lax.all_gather(frontier, 'row', axis=0, tiled=True)  259 us
    psum x6, blocking collectives, local(): squares = lax.psum(jnp.sum(raw_paths * raw_paths, axis=0), ('row', 'col'))  242 us
    reduce_scatter x6, waiting for transfers between devices, local(): lax.psum_scatter(combined.reshape(dest_tiles * TILE, panel_width), 'col',...  132 us
    scatter-add x24, other arithmetic, one_turn(): summed.at[part_rows]  38.3 us
    dot_general x24, matrix products, one_turn(): jnp.einsum('gij,gjs->gis', part_blocks, picked, preferred_element_type=jn...  34.1 us
    and x24, other arithmetic, one_turn(): picked = jnp.take(sources, local_cols, axis=0)  17.2 us
    another operation x6, loops' own time, tile_products(): return lax.fori_loop(0, turn_count, one_turn, running)  17.1 us
  transfers between devices with their start and end apart: 6, of which 6 were waited for; matrix products, arithmetic and copies ran while one was open for 0% of the time, Pallas kernels for 0%

commit v1 on v0

v1 whole, which is shorter than its diff:
```python
import functools
import math

import jax
import jax.numpy as jnp
from jax import lax
from jax.experimental import pallas as pl
from jax.experimental.pallas import tpu as pltpu
from jax.sharding import PartitionSpec as P

TILE = 128
LEVELS = 6
EPSILON = 1e-06
CHUNK = 16
MESH = pl.DeviceIdType.MESH


def build_kernel(count_ref, rows_ref, cols_ref, adj_ref, dense_ref, blocks, sems):
    slots = adj_ref.shape[0]
    chunk = math.gcd(CHUNK, slots)
    count = count_ref[0]

    def fetch(index):
        return pltpu.make_async_copy(
            adj_ref.at[pl.ds(index * chunk, chunk)], blocks.at[pl.ds(index * chunk, chunk)], sems.at[index]
        )

    for index in range(slots // chunk):
        @pl.when(index * chunk < count)
        def _():
            fetch(index).start()

    dense_ref[...] = jnp.zeros_like(dense_ref)

    for index in range(slots // chunk):
        @pl.when(index * chunk < count)
        def _():
            fetch(index).wait()

            def add(slot, carry):
                row = pl.multiple_of(rows_ref[slot] * TILE, TILE)
                col = pl.multiple_of(cols_ref[slot] * TILE, TILE)
                where = (pl.ds(row, TILE), pl.ds(col, TILE))
                dense_ref[where] = dense_ref[where] + blocks[slot]
                return carry

            lax.fori_loop(index * chunk, jnp.minimum(count, (index + 1) * chunk), add, 0)


def build(adj, rows, cols, count, dest_tiles, src_tiles):
    slots = adj.shape[0]
    smem = pl.BlockSpec(memory_space=pltpu.SMEM)
    return pl.pallas_call(
        build_kernel,
        out_shape=jax.ShapeDtypeStruct((dest_tiles * TILE, src_tiles * TILE), adj.dtype),
        in_specs=[smem, smem, smem, pl.BlockSpec(memory_space=pl.ANY)],
        out_specs=pl.BlockSpec(memory_space=pltpu.VMEM),
        scratch_shapes=[
            pltpu.VMEM(adj.shape, adj.dtype),
            pltpu.SemaphoreType.DMA((slots // math.gcd(CHUNK, slots),)),
        ],
        compiler_params=pltpu.CompilerParams(vmem_limit_bytes=40 * 1024 * 1024),
        name="build_dense",
    )(count, rows, cols, adj)


def level_kernel(
    row_total, col_total, inner,
    dense_ref, depth_ref, source_ref, sums_ref, logs_ref,
    panel, partial, squares, raw, depths,
    panel_send, panel_recv, part_send, part_recv, square_send, square_recv, depth_send, depth_recv,
):
    me_row, me_col = lax.axis_index("row"), lax.axis_index("col")
    piece = sums_ref.shape[0]
    piece_tiles = depth_ref.shape[0]
    half = piece // 2
    vertex_total = piece * row_total * col_total
    outer = row_total // inner
    my_inner, my_outer = lax.rem(me_row, inner), lax.div(me_row, inner)
    row_peers = [lax.rem(me_row + step, row_total) for step in range(1, row_total)]
    col_peers = [lax.rem(me_col + step, col_total) for step in range(1, col_total)]
    inner_peers = [lax.rem(my_inner + step, inner) for step in range(1, inner)]
    outer_peers = [lax.rem(my_outer + step, outer) for step in range(1, outer)]

    barrier = pltpu.get_barrier_semaphore()
    for peer in row_peers:
        pl.semaphore_signal(barrier, inc=1, device_id=(peer, me_col), device_id_type=MESH)
    for peer in col_peers:
        pl.semaphore_signal(barrier, inc=1, device_id=(me_row, peer), device_id_type=MESH)

    sources = source_ref[...]
    offsets = lax.broadcasted_iota(jnp.int32, (piece, sources.shape[1]), 0)
    for row in range(row_total):
        first = (row * col_total + me_col) * piece
        panel[0, row] = (offsets + first == sources).astype(jnp.float32).astype(panel.dtype)
    mine = (offsets + (me_row * col_total + me_col) * piece == sources).astype(jnp.float32)
    sums_ref[...] = mine
    depths[pl.ds(me_col, 1)] = depth_ref[...][None]

    def product(slot):
        whole = panel[slot].reshape(row_total * piece, panel.shape[3])
        return jnp.dot(dense_ref[...], whole, preferred_element_type=jnp.float32)

    def copies(source, target, send, recv, peers):
        return [
            pltpu.make_async_remote_copy(
                src_ref=source, dst_ref=target, send_sem=send(step), recv_sem=recv,
                device_id=peer, device_id_type=MESH,
            )
            for step, peer in enumerate(peers)
        ]

    def arrival(target, recv):
        return pltpu.make_async_copy(target, target, recv)

    def total_square(slot):
        mean_square = jnp.sum(squares[slot], axis=0) / vertex_total + EPSILON
        return mean_square

    panel_sends, square_sends, part_sends, depth_sends = [], [], [], []
    scale = None
    for level in range(1, LEVELS + 1):
        slot = level % 2
        before = (level + 1) % 2
        if level > 1:
            for group_step, peer in enumerate(inner_peers):
                owner = my_outer * inner + peer
                place = panel.at[before, owner, pl.ds(0, half)]
                arrival(place, panel_recv.at[before, owner, 0]).wait()
                base = inner - 1 + (group_step + 1) * (outer - 1)
                sends = copies(
                    place, place, lambda step: panel_send.at[0, base + step], panel_recv.at[before, owner, 0],
                    [(other * inner + my_inner, me_col) for other in outer_peers],
                )
                for copy in sends:
                    copy.start()
                panel_sends += sends
            for group_step, peer in enumerate(outer_peers):
                owner = peer * inner + my_inner
                place = panel.at[before, owner, pl.ds(half, piece - half)]
                arrival(place, panel_recv.at[before, owner, 1]).wait()
                base = outer - 1 + (group_step + 1) * (inner - 1)
                sends = copies(
                    place, place, lambda step: panel_send.at[1, base + step], panel_recv.at[before, owner, 1],
                    [(my_outer * inner + other, me_col) for other in inner_peers],
                )
                for copy in sends:
                    copy.start()
                panel_sends += sends
            for peer_outer in outer_peers:
                for peer_inner in [my_inner] + inner_peers:
                    owner = peer_outer * inner + peer_inner
                    place = panel.at[before, owner, pl.ds(0, half)]
                    arrival(place, panel_recv.at[before, owner, 0]).wait()
            for peer_inner in inner_peers:
                for peer_outer in [my_outer] + outer_peers:
                    owner = peer_outer * inner + peer_inner
                    place = panel.at[before, owner, pl.ds(half, piece - half)]
                    arrival(place, panel_recv.at[before, owner, 1]).wait()
        partial[slot, pl.ds(me_col, 1)] = product(before)[None]
        if level == 1:
            pl.semaphore_wait(barrier, row_total + col_total - 2)
            depth_sends = copies(
                depth_ref, depths.at[me_col], lambda step: depth_send.at[step], depth_recv.at[me_col],
                [(me_row, peer) for peer in col_peers],
            )
            for copy in depth_sends:
                copy.start()
        for copy in part_sends:
            copy.wait_send()
        part_sends = copies(
            partial.at[slot, me_col], partial.at[slot, me_col],
            lambda step: part_send.at[step], part_recv.at[slot, me_col],
            [(me_row, peer) for peer in col_peers],
        )
        for copy in part_sends:
            copy.start()
        for copy in panel_sends + square_sends:
            copy.wait_send()
        panel_sends, square_sends = [], []
        if level > 1:
            for peer in row_peers:
                arrival(squares.at[before, peer], square_recv.at[before, peer]).wait()
            mean_square = total_square(before)
            scale = lax.rsqrt(mean_square)
            logs_ref[level - 2 : level - 1] = 0.5 * jnp.log(mean_square)
            sums_ref[...] = sums_ref[...] + raw[me_col] * scale
        for peer in col_peers:
            arrival(partial.at[slot, peer], part_recv.at[slot, peer]).wait()
            if level == 1:
                arrival(depths.at[peer], depth_recv.at[peer]).wait()
        summed = partial[slot, 0]
        for col in range(1, col_total):
            summed = summed + partial[slot, col]
        reached = (depths[...] >= level).astype(jnp.float32)
        if level > 1:
            reached = reached * scale
        tiles = summed.reshape(col_total * piece_tiles, TILE, summed.shape[1])
        tiles = tiles * reached.reshape(col_total * piece_tiles, 1, summed.shape[1])
        raw[...] = tiles.reshape(raw.shape)
        if level < LEVELS:
            panel[slot, pl.ds(me_row, 1)] = raw[pl.ds(me_col, 1)].astype(panel.dtype)
            place = panel.at[slot, me_row, pl.ds(0, half)]
            panel_sends += copies(
                place, place, lambda step: panel_send.at[0, step], panel_recv.at[slot, me_row, 0],
                [(my_outer * inner + other, me_col) for other in inner_peers]
                + [(other * inner + my_inner, me_col) for other in outer_peers],
            )
            place = panel.at[slot, me_row, pl.ds(half, piece - half)]
            panel_sends += copies(
                place, place, lambda step: panel_send.at[1, step], panel_recv.at[slot, me_row, 1],
                [(other * inner + my_inner, me_col) for other in outer_peers]
                + [(my_outer * inner + other, me_col) for other in inner_peers],
            )
            for copy in panel_sends:
                copy.start()
        flat = tiles.reshape(col_total * piece, summed.shape[1])
        squares[slot, pl.ds(me_row, 1)] = jnp.sum(flat * flat, axis=0, keepdims=True)[None]
        square_sends = copies(
            squares.at[slot, me_row], squares.at[slot, me_row],
            lambda step: square_send.at[step], square_recv.at[slot, me_row],
            [(peer, me_col) for peer in row_peers],
        )
        for copy in square_sends:
            copy.start()
    last = LEVELS % 2
    for peer in row_peers:
        arrival(squares.at[last, peer], square_recv.at[last, peer]).wait()
    mean_square = total_square(last)
    logs_ref[LEVELS - 1 : LEVELS] = 0.5 * jnp.log(mean_square)
    sums_ref[...] = sums_ref[...] + raw[me_col] * lax.rsqrt(mean_square)
    for copy in part_sends + square_sends + depth_sends:
        copy.wait_send()


def inner_size(total):
    return max(size for size in range(1, total + 1) if total % size == 0 and size * size <= total)


def levels(dense, depth, source_ids, row_total, col_total):
    piece_tiles, width = depth.shape
    piece = piece_tiles * TILE
    inner = inner_size(row_total)
    vmem = pl.BlockSpec(memory_space=pltpu.VMEM)
    dma = pltpu.SemaphoreType.DMA
    return pl.pallas_call(
        functools.partial(level_kernel, row_total, col_total, inner),
        out_shape=(
            jax.ShapeDtypeStruct((piece, width), jnp.float32),
            jax.ShapeDtypeStruct((LEVELS, width), jnp.float32),
        ),
        in_specs=[vmem, vmem, vmem],
        out_specs=(vmem, vmem),
        scratch_shapes=[
            pltpu.VMEM((2, row_total, piece, width), jnp.bfloat16),
            pltpu.VMEM((2, col_total, col_total * piece, width), jnp.float32),
            pltpu.VMEM((2, row_total, 1, width), jnp.float32),
            pltpu.VMEM((col_total, piece, width), jnp.float32),
            pltpu.VMEM((col_total, piece_tiles, width), jnp.int32),
            dma((2, row_total)),
            dma((2, row_total, 2)),
            dma((col_total,)),
            dma((2, col_total)),
            dma((row_total,)),
            dma((2, row_total)),
            dma((col_total,)),
            dma((col_total,)),
        ],
        compiler_params=pltpu.CompilerParams(
            collective_id=0, has_side_effects=True, vmem_limit_bytes=56 * 1024 * 1024
        ),
        name="levels",
    )(dense, depth, source_ids)


def local(adj_tiles, tile_rows, tile_cols, tile_count, tile_depth, source_ids):
    row_total, col_total = lax.axis_size("row"), lax.axis_size("col")
    piece_tiles, width = tile_depth.shape
    dense = build(
        adj_tiles[0, 0], tile_rows[0, 0], tile_cols[0, 0], tile_count[0], col_total * piece_tiles, row_total * piece_tiles
    )
    return levels(dense, tile_depth, source_ids.reshape(1, width), row_total, col_total)


def solution(mesh):
    in_specs = (
        P("row", "col", None, None, None),
        P("row", "col", None),
        P("row", "col", None),
        P("row", "col"),
        P(("row", "col"), None),
        P(),
    )
    out_specs = (P(("row", "col"), None), P())
    return jax.shard_map(local, mesh=mesh, in_specs=in_specs, out_specs=out_specs, check_vma=False)
```

time: 810 us -> 81.2 us (0.10)
  blocking collectives: 501 us -> 0 us
  waiting for transfers between devices: 132 us -> 0 us
  other arithmetic: 77.3 us -> 0 us
  Pallas kernels: 0 us -> 71.7 us
  matrix products: 34.1 us -> 0 us
  local copies, waits for them, and re-layouts: 27.7 us -> 7.19 us
  loops' own time: 17.1 us -> 0 us
  between operations: 16.3 us -> 1.31 us
    all_gather x6 -> x0, blocking collectives: 259 us -> none  [local(): piece_block = lax.all_gather(frontier, 'row', axis=0, tiled=True)]
    psum x6 -> x0, blocking collectives: 242 us -> none  [local(): squares = lax.psum(jnp.sum(raw_paths * raw_paths, axis=0), ('row', 'col'))]
    reduce_scatter x6 -> x0, waiting for transfers between devices: 132 us -> none  [local(): lax.psum_scatter(combined.reshape(dest_tiles * TILE, panel_width), 'col',...]
    pallas_call x0 -> x2, Pallas kernels: none -> 71.7 us  [the longest x1 70.2 us: levels(): pl.pallas_call(functools.partial(level_kernel, row_total, col_total, inne...]
    scatter-add x24 -> x0, other arithmetic: 38.3 us -> none  [one_turn(): summed.at[part_rows]]
    dot_general x24 -> x0, matrix products: 34.1 us -> none  [one_turn(): jnp.einsum('gij,gjs->gis', part_blocks, picked, preferred_element_type=jn...]
    gather x27 -> x0, local copies, waits for them, and re-layouts: 23.2 us -> none  [the longest x24 15.6 us: one_turn(): picked = jnp.take(sources, local_cols, axis=0)]
    and x24 -> x0, other arithmetic: 17.2 us -> none  [one_turn(): picked = jnp.take(sources, local_cols, axis=0)]
  transfers between devices with their start and end apart: 6 -> 0, of which waited for: 6 -> 0; matrix products, arithmetic and copies ran while one was open for 0% -> 0% of each run, Pallas kernels for 0% -> 0%
where the time goes in v1:
time: 81.2 us; the launch traced here: 80.2 us
  Pallas kernels  71.7 us (88%)
  local copies, waits for them, and re-layouts  7.19 us (9%)
  between operations  1.31 us (2%)
    pallas_call x1, Pallas kernels, levels(): pl.pallas_call(functools.partial(level_kernel, row_total, col_total, inne...  70.2 us
    unnamed x10, local copies, waits for them, and re-layouts  7.19 us

profile of v1, /device:TPU:0, one launch (start us, length us, event | category | flops | bytes accessed | tf_op | source)
XLA Modules:
  0.0 80.2 jit_solution(4008900592981300548)
XLA Ops:
  1.3 0.0 copy-start
  1.3 2.2 %copy-done = bf16[1,1,128,128,128]{4,3,2,1,0:T(8,128)(2,1)S(1)} copy-done((bf16[1,1,128,128,128]{4,3,2,1,0:T(8,128)(2,1)S(1)}, bf16[1,1,128,128,128]{4,3,2,1,0:T(8,128)(2,1)}, u32[]{:S(2)}) %copy-start) | copy-done | bytes 4194328
  3.5 0.0 copy-start.2
  3.5 0.7 copy-done.2
  4.1 0.0 copy-start.3
  4.1 0.7 copy-done.3
  4.8 1.5 %build_dense.1.dense_ref = bf16[256,2048]{1,0:T(8,128)(2,1)S(1)} custom-call(s32[1]{0:T(128)} %bitcast.5.count_ref, s32[128]{0:T(128)S(1)} %bitcast.7, s32[128]{0:T(128)S(1)} %bitcast.8, bf16[128,128,128]{2,1,0:T(8,128)(2,1)S(1)} %bitcast.6), custom_call_target="tpu_custom_call" | custom-call | tf_op jit(solution)/shard_map/build_dense/pallas_call | solution.py:53
  6.2 0.0 copy-start.1
  6.3 1.0 %copy-done.1 = bf16[256,2048]{1,0:T(8,128)(2,1)} copy-done((bf16[256,2048]{1,0:T(8,128)(2,1)}, bf16[256,2048]{1,0:T(8,128)(2,1)S(1)}, u32[]{:S(2)}) %copy-start.1) | copy-done | bytes 1048600
  7.2 70.2 %levels.1 = (f32[128,128]{1,0:T(8,128)}, f32[6,128]{1,0:T(8,128)}) custom-call(bf16[256,2048]{1,0:T(8,128)(2,1)} %copy-done.1, s32[1,128]{1,0:T(1,128)} %depth_ref.1, s32[1,128]{1,0:T(1,128)} %bitcast.9), custom_call_target="tpu_custom_call" | custom-call | tf_op jit(solution)/shard_map/levels/pallas_call | solution.py:246
  77.4 1.5 %copy.11 = f32[128,128]{1,0:T(8,128)} copy(f32[128,128]{1,0:T(8,128)} %get-tuple-element.4) | data formatting | bytes 131072
  78.9 1.3 %copy.12 = f32[6,128]{1,0:T(8,128)} copy(f32[6,128]{1,0:T(8,128)} %get-tuple-element.5) | data formatting | bytes 6144
Async XLA Ops:
  1.3 2.2 %copy-start = (bf16[1,1,128,128,128]{4,3,2,1,0:T(8,128)(2,1)S(1)}, bf16[1,1,128,128,128]{4,3,2,1,0:T(8,128)(2,1)}, u32[]{:S(2)}) copy-start(bf16[1,1,128,128,128]{4,3,2,1,0:T(8,128)(2,1)} %param.6) | copy-start | bytes 12582916
  3.5 0.7 copy-start.2
  4.1 0.7 copy-start.3
  6.2 1.0 %copy-start.1 = (bf16[256,2048]{1,0:T(8,128)(2,1)}, bf16[256,2048]{1,0:T(8,128)(2,1)S(1)}, u32[]{:S(2)}) copy-start(bf16[256,2048]{1,0:T(8,128)(2,1)S(1)} %build_dense.1.dense_ref) | copy-start | bytes 3145732

commit v2 on v1

--- a/solution.py
+++ b/solution.py
@@ -12,10 +12,11 @@
 LEVELS = 6
 EPSILON = 1e-06
 CHUNK = 16
+SPLIT_NUM = 4
 MESH = pl.DeviceIdType.MESH
 
 
-def build_kernel(count_ref, rows_ref, cols_ref, adj_ref, dense_ref, blocks, sems):
+def build_kernel(count_ref, rows_hbm, cols_hbm, adj_ref, dense_ref, blocks, rows_ref, cols_ref, sems, list_sems):
     slots = adj_ref.shape[0]
     chunk = math.gcd(CHUNK, slots)
     count = count_ref[0]
@@ -25,12 +26,20 @@
             adj_ref.at[pl.ds(index * chunk, chunk)], blocks.at[pl.ds(index * chunk, chunk)], sems.at[index]
         )
 
+    lists = [
+        pltpu.make_async_copy(rows_hbm, rows_ref, list_sems.at[0]),
+        pltpu.make_async_copy(cols_hbm, cols_ref, list_sems.at[1]),
+    ]
+    for copy in lists:
+        copy.start()
     for index in range(slots // chunk):
         @pl.when(index * chunk < count)
         def _():
             fetch(index).start()
 
     dense_ref[...] = jnp.zeros_like(dense_ref)
+    for copy in lists:
+        copy.wait()
 
     for index in range(slots // chunk):
         @pl.when(index * chunk < count)
@@ -49,39 +58,58 @@
 
 def build(adj, rows, cols, count, dest_tiles, src_tiles):
     slots = adj.shape[0]
-    smem = pl.BlockSpec(memory_space=pltpu.SMEM)
+    smem, hbm = pl.BlockSpec(memory_space=pltpu.SMEM), pl.BlockSpec(memory_space=pl.ANY)
     return pl.pallas_call(
         build_kernel,
         out_shape=jax.ShapeDtypeStruct((dest_tiles * TILE, src_tiles * TILE), adj.dtype),
-        in_specs=[smem, smem, smem, pl.BlockSpec(memory_space=pl.ANY)],
+        in_specs=[smem, hbm, hbm, hbm],
         out_specs=pl.BlockSpec(memory_space=pltpu.VMEM),
         scratch_shapes=[
             pltpu.VMEM(adj.shape, adj.dtype),
+            pltpu.SMEM(rows.shape, rows.dtype),
+            pltpu.SMEM(cols.shape, cols.dtype),
             pltpu.SemaphoreType.DMA((slots // math.gcd(CHUNK, slots),)),
+            pltpu.SemaphoreType.DMA((2,)),
         ],
         compiler_params=pltpu.CompilerParams(vmem_limit_bytes=40 * 1024 * 1024),
         name="build_dense",
     )(count, rows, cols, adj)
 
 
+def mirrored(me, size):
+    if size & (size - 1):
+        return [lax.rem(me + step, size) for step in range(1, size)]
+    peers = []
+    for step in range(1, size):
+        peer = me
+        for bit in range(size.bit_length()):
+            if step >> bit & 1:
+                peer = peer + (1 << bit) * (1 - 2 * lax.rem(lax.div(me, 1 << bit), 2))
+        peers.append(peer)
+    return peers
+
+
 def level_kernel(
     row_total, col_total, inner,
-    dense_ref, depth_ref, source_ref, sums_ref, logs_ref,
-    panel, partial, squares, raw, depths,
+    dense_hbm, depth_ref, source_ref, sums_ref, logs_ref,
+    dense_ref, dense_sem, panel, partial, squares, raw, depths,
     panel_send, panel_recv, part_send, part_recv, square_send, square_recv, depth_send, depth_recv,
 ):
     me_row, me_col = lax.axis_index("row"), lax.axis_index("col")
     piece = sums_ref.shape[0]
     piece_tiles = depth_ref.shape[0]
-    half = piece // 2
+    half = piece * SPLIT_NUM // 8
     vertex_total = piece * row_total * col_total
     outer = row_total // inner
     my_inner, my_outer = lax.rem(me_row, inner), lax.div(me_row, inner)
     row_peers = [lax.rem(me_row + step, row_total) for step in range(1, row_total)]
     col_peers = [lax.rem(me_col + step, col_total) for step in range(1, col_total)]
-    inner_peers = [lax.rem(my_inner + step, inner) for step in range(1, inner)]
-    outer_peers = [lax.rem(my_outer + step, outer) for step in range(1, outer)]
-
+    inner_peers = mirrored(my_inner, inner)
+    steps = sorted(range(1, outer), key=lambda step: min(step, outer - step))
+    outer_peers = [lax.rem(my_outer + step, outer) for step in steps]
+
+    dense_copy = pltpu.make_async_copy(dense_hbm, dense_ref, dense_sem)
+    dense_copy.start()
     barrier = pltpu.get_barrier_semaphore()
     for peer in row_peers:
         pl.semaphore_signal(barrier, inc=1, device_id=(peer, me_col), device_id_type=MESH)
@@ -97,9 +125,11 @@
     sums_ref[...] = mine
     depths[pl.ds(me_col, 1)] = depth_ref[...][None]
 
-    def product(slot):
-        whole = panel[slot].reshape(row_total * piece, panel.shape[3])
-        return jnp.dot(dense_ref[...], whole, preferred_element_type=jnp.float32)
+    def product(slot, group):
+        span = inner * piece
+        block = panel[slot, pl.ds(group * inner, inner)].reshape(span, panel.shape[3])
+        columns = dense_ref[:, pl.ds(pl.multiple_of(group * span, span), span)]
+        return jnp.dot(columns, block, preferred_element_type=jnp.float32)
 
     def copies(source, target, send, recv, peers):
         return [
@@ -123,41 +153,43 @@
         slot = level % 2
         before = (level + 1) % 2
         if level > 1:
-            for group_step, peer in enumerate(inner_peers):
-                owner = my_outer * inner + peer
-                place = panel.at[before, owner, pl.ds(0, half)]
-                arrival(place, panel_recv.at[before, owner, 0]).wait()
-                base = inner - 1 + (group_step + 1) * (outer - 1)
+            turns = [(step, 0, peer) for step, peer in enumerate(inner_peers)]
+            turns += [(step, 1, peer) for step, peer in enumerate(outer_peers)]
+            for group_step, part_index, peer in sorted(turns, key=lambda turn: turn[:2]):
+                if part_index == 0:
+                    owner = my_outer * inner + peer
+                    rows = pl.ds(0, half)
+                    targets = [(other * inner + my_inner, me_col) for other in outer_peers]
+                    base = inner - 1 + (group_step + 1) * (outer - 1)
+                else:
+                    owner = peer * inner + my_inner
+                    rows = pl.ds(half, piece - half)
+                    targets = [(my_outer * inner + other, me_col) for other in inner_peers]
+                    base = outer - 1 + (group_step + 1) * (inner - 1)
+                place = panel.at[before, owner, rows]
+                arrival(place, panel_recv.at[before, owner, part_index]).wait()
                 sends = copies(
-                    place, place, lambda step: panel_send.at[0, base + step], panel_recv.at[before, owner, 0],
-                    [(other * inner + my_inner, me_col) for other in outer_peers],
+                    place, place, lambda step: panel_send.at[part_index, base + step],
+                    panel_recv.at[before, owner, part_index], targets,
                 )
                 for copy in sends:
                     copy.start()
                 panel_sends += sends
-            for group_step, peer in enumerate(outer_peers):
-                owner = peer * inner + my_inner
-                place = panel.at[before, owner, pl.ds(half, piece - half)]
-                arrival(place, panel_recv.at[before, owner, 1]).wait()
-                base = outer - 1 + (group_step + 1) * (inner - 1)
-                sends = copies(
-                    place, place, lambda step: panel_send.at[1, base + step], panel_recv.at[before, owner, 1],
-                    [(my_outer * inner + other, me_col) for other in inner_peers],
-                )
-                for copy in sends:
-                    copy.start()
-                panel_sends += sends
-            for peer_outer in outer_peers:
+        else:
+            dense_copy.wait()
+        total = None
+        for group in [my_outer] + outer_peers:
+            if level > 1:
                 for peer_inner in [my_inner] + inner_peers:
-                    owner = peer_outer * inner + peer_inner
-                    place = panel.at[before, owner, pl.ds(0, half)]
-                    arrival(place, panel_recv.at[before, owner, 0]).wait()
-            for peer_inner in inner_peers:
-                for peer_outer in [my_outer] + outer_peers:
-                    owner = peer_outer * inner + peer_inner
-                    place = panel.at[before, owner, pl.ds(half, piece - half)]
-                    arrival(place, panel_recv.at[before, owner, 1]).wait()
-        partial[slot, pl.ds(me_col, 1)] = product(before)[None]
+                    owner = group * inner + peer_inner
+                    if group is not my_outer:
+                        arrival(panel.at[before, owner, pl.ds(0, half)], panel_recv.at[before, owner, 0]).wait()
+                    if peer_inner is not my_inner:
+                        place = panel.at[before, owner, pl.ds(half, piece - half)]
+                        arrival(place, panel_recv.at[before, owner, 1]).wait()
+            part = product(before, group)
+            total = part if total is None else total + part
+        partial[slot, pl.ds(me_col, 1)] = total[None]
         if level == 1:
             pl.semaphore_wait(barrier, row_total + col_total - 2)
             depth_sends = copies(
@@ -249,9 +281,11 @@
             jax.ShapeDtypeStruct((piece, width), jnp.float32),
             jax.ShapeDtypeStruct((LEVELS, width), jnp.float32),
         ),
-        in_specs=[vmem, vmem, vmem],
+        in_specs=[pl.BlockSpec(memory_space=pl.ANY), vmem, vmem],
         out_specs=(vmem, vmem),
         scratch_shapes=[
+            pltpu.VMEM(dense.shape, dense.dtype),
+            pltpu.SemaphoreType.DMA,
             pltpu.VMEM((2, row_total, piece, width), jnp.bfloat16),
             pltpu.VMEM((2, col_total, col_total * piece, width), jnp.float32),
             pltpu.VMEM((2, row_total, 1, width), jnp.float32),
@@ -273,13 +307,29 @@
     )(dense, depth, source_ids)
 
 
+def finish_kernel(sums_in, logs_in, sums_out, logs_out):
+    sums_out[...] = sums_in[...]
+    logs_out[...] = logs_in[...]
+
+
+def finish(sums, logs):
+    vmem = pl.BlockSpec(memory_space=pltpu.VMEM)
+    return pl.pallas_call(
+        finish_kernel,
+        out_shape=(jax.ShapeDtypeStruct(sums.shape, sums.dtype), jax.ShapeDtypeStruct(logs.shape, logs.dtype)),
+        in_specs=[vmem, vmem],
+        out_specs=(vmem, vmem),
+        name="finish",
+    )(sums, logs)
+
+
 def local(adj_tiles, tile_rows, tile_cols, tile_count, tile_depth, source_ids):
     row_total, col_total = lax.axis_size("row"), lax.axis_size("col")
     piece_tiles, width = tile_depth.shape
     dense = build(
         adj_tiles[0, 0], tile_rows[0, 0], tile_cols[0, 0], tile_count[0], col_total * piece_tiles, row_total * piece_tiles
     )
-    return levels(dense, tile_depth, source_ids.reshape(1, width), row_total, col_total)
+    return finish(*levels(dense, tile_depth, source_ids.reshape(1, width), row_total, col_total))
 
 
 def solution(mesh):

time: 81.2 us -> 77.2 us (0.951); the launches traced: 80.2 us -> 77.4 us
  local copies, waits for them, and re-layouts: 7.19 us -> 4.45 us
    unnamed x10 -> x8, local copies, waits for them, and re-layouts: 7.19 us -> 4.45 us
    pallas_call x1, Pallas kernels: 70.2 us -> 68.5 us  [levels(): pl.pallas_call(functools.partial(level_kernel, row_total, col_total, inne...]
    pallas_call x0 -> x1, Pallas kernels: none -> 1.48 us  [finish(): pl.pallas_call(finish_kernel, out_shape=(jax.ShapeDtypeStruct(sums.shape,...]
where the time goes in v2:
time: 77.2 us; the launch traced here: 77.4 us
  Pallas kernels  71.7 us (93%)
  local copies, waits for them, and re-layouts  4.45 us (6%)
  between operations  1.31 us (2%)
    pallas_call x1, Pallas kernels, levels(): pl.pallas_call(functools.partial(level_kernel, row_total, col_total, inne...  68.5 us
    unnamed x8, local copies, waits for them, and re-layouts  4.45 us
    pallas_call x1, Pallas kernels, build(): pl.pallas_call(build_kernel, out_shape=jax.ShapeDtypeStruct((dest_tiles *...  1.66 us

profile of v2, /device:TPU:0, one launch (start us, length us, event | category | flops | bytes accessed | tf_op | source)
XLA Modules:
  0.0 77.4 jit_solution(5033353300211040181)
XLA Ops:
  1.3 0.0 copy-start
  1.3 2.2 %copy-done = bf16[1,1,128,128,128]{4,3,2,1,0:T(8,128)(2,1)S(1)} copy-done((bf16[1,1,128,128,128]{4,3,2,1,0:T(8,128)(2,1)S(1)}, bf16[1,1,128,128,128]{4,3,2,1,0:T(8,128)(2,1)}, u32[]{:S(2)}) %copy-start) | copy-done | bytes 4194328
  3.5 0.0 copy-start.2
  3.5 0.7 copy-done.2
  4.1 0.0 copy-start.3
  4.1 0.7 copy-done.3
  4.8 1.7 %build_dense.1.dense_hbm = bf16[256,2048]{1,0:T(8,128)(2,1)S(1)} custom-call(s32[1]{0:T(128)} %bitcast.5.count_ref, s32[128]{0:T(128)S(1)} %bitcast.7, s32[128]{0:T(128)S(1)} %bitcast.8, bf16[128,128,128]{2,1,0:T(8,128)(2,1)S(1)} %bitcast.6), custom_call_target="tpu_custom_call" | custom-call | tf_op jit(solution)/shard_map/build_dense/pallas_call | solution.py:62
  6.4 0.0 copy-start.1
  6.5 1.0 %copy-done.1 = bf16[256,2048]{1,0:T(8,128)(2,1)} copy-done((bf16[256,2048]{1,0:T(8,128)(2,1)}, bf16[256,2048]{1,0:T(8,128)(2,1)S(1)}, u32[]{:S(2)}) %copy-start.1) | copy-done | bytes 1048600
  7.4 68.5 %levels.1 = (f32[128,128]{1,0:T(8,128)}, f32[6,128]{1,0:T(8,128)}) custom-call(bf16[256,2048]{1,0:T(8,128)(2,1)} %copy-done.1, s32[1,128]{1,0:T(1,128)} %depth_ref.1, s32[1,128]{1,0:T(1,128)} %bitcast.9), custom_call_target="tpu_custom_call" | custom-call | tf_op jit(solution)/shard_map/levels/pallas_call | solution.py:278
  76.0 1.5 %finish.1 = (f32[128,128]{1,0:T(8,128)}, f32[6,128]{1,0:T(8,128)}) custom-call(f32[128,128]{1,0:T(8,128)} %get-tuple-element.4.sums_in, f32[6,128]{1,0:T(8,128)} %get-tuple-element.5.logs_in), custom_call_target="tpu_custom_call" | custom-call | tf_op jit(solution)/shard_map/finish/pallas_call | solution.py:317
Async XLA Ops:
  1.3 2.2 %copy-start = (bf16[1,1,128,128,128]{4,3,2,1,0:T(8,128)(2,1)S(1)}, bf16[1,1,128,128,128]{4,3,2,1,0:T(8,128)(2,1)}, u32[]{:S(2)}) copy-start(bf16[1,1,128,128,128]{4,3,2,1,0:T(8,128)(2,1)} %param.6) | copy-start | bytes 12582916
  3.5 0.7 copy-start.2
  4.1 0.7 copy-start.3
  6.4 1.0 %copy-start.1 = (bf16[256,2048]{1,0:T(8,128)(2,1)}, bf16[256,2048]{1,0:T(8,128)(2,1)S(1)}, u32[]{:S(2)}) copy-start(bf16[256,2048]{1,0:T(8,128)(2,1)S(1)} %build_dense.1.dense_hbm) | copy-start | bytes 3145732
